TPU v7x, 32 devices: a whole 2x2x4 slice. The times are simulated.
32 devices in a mesh: gx: 4 (over z), gy: 4 (over y, core), gz: 2 (over x).
Axes of the slice: x: 2, y: 2, z: 4, core: 2. Of those that a mesh axis runs over, the one named last changes fastest.
Arguments:
- right_side: float32 [128, 128, 256], P('gx', 'gy', 'gz'), may hold values from -8 to 8
- guess: float32 [128, 128, 256], P('gx', 'gy', 'gz'), may hold values from -4 to 4
Outputs:
- solution_field: float32 [128, 128, 256], P('gx', 'gy', 'gz')
- residual: float32 [128, 128, 256], P('gx', 'gy', 'gz')
All inputs are finite; a program needn't handle non-finite values.
Results may differ from a plain program's by a relative error of at most 0.0001.
Values sent between devices are 32-bit elements; how exact they have to be, the bound alone decides.
A program may use at most 128 MiB of HBM per device.

v0:
```python
import jax
import jax.numpy as jnp
from jax import lax
from jax.sharding import PartitionSpec as P

LEVELS = 6
SWEEPS = 4
STEPS = 2
damping = 2.0 / 3.0


def passed_along(value, axis, steps):
    count = lax.axis_size(axis)
    first, last = (max(0, -steps), min(count, count - steps))
    return lax.ppermute(value, axis, [(source, source + steps) for source in range(first, last)])


def padded_2(x, sides, width):
    for axis, dim in sides:
        count, length = (lax.axis_size(axis), x.shape[dim])
        up = [(i, (i + 1) % count) for i in range(count - 1)]
        down = [(j, i) for i, j in up]
        last = lax.slice_in_dim(x, length - width, length, axis=dim)
        first = lax.slice_in_dim(x, 0, width, axis=dim)
        before = lax.ppermute(last, axis, up)
        after = lax.ppermute(first, axis, down)
        x = jnp.concatenate([before, x, after], axis=dim)
    return x


def padded_stencil(padded):
    beside = padded[2:, 1:-1, 1:-1] + padded[:-2, 1:-1, 1:-1]
    beside = beside + padded[1:-1, 2:, 1:-1] + padded[1:-1, :-2, 1:-1]
    beside = beside + padded[1:-1, 1:-1, 2:] + padded[1:-1, 1:-1, :-2]
    return 6.0 * padded[1:-1, 1:-1, 1:-1] - beside


def restrict(field):
    first, second, third = field.shape
    blocks = field.reshape(first // 2, 2, second // 2, 2, third // 2, 2)
    return jnp.mean(blocks, axis=(1, 3, 5))


def prolong(field):
    first, second, third = field.shape
    spread = jnp.broadcast_to(field[:, None, :, None, :, None], (first, 2, second, 2, third, 2))
    return spread.reshape(first * 2, second * 2, third * 2)


def axis_layers(packed, axis_name, by):
    if axis_name == "gx":
        return passed_along(packed, "gx", by)
    if axis_name == "gy":
        return passed_along(packed, "gy", by)
    return passed_along(packed, "gz", by)


def extend_all(fields, margin):
    current = list(fields)
    for dim_index, axis_name in ((0, "gx"), (1, "gy"), (2, "gz")):
        lows = [lax.slice_in_dim(f, 0, margin, axis=dim_index) for f in current]
        highs = [
            lax.slice_in_dim(f, f.shape[dim_index] - margin, f.shape[dim_index], axis=dim_index)
            for f in current
        ]
        received = {}
        for by in (1, -1):
            pieces = highs if by == 1 else lows
            packed = jnp.concatenate([p.reshape(-1) for p in pieces])
            received[by] = axis_layers(packed, axis_name, by)
        grown = []
        offset = 0
        for index, field in enumerate(current):
            piece_shape = lows[index].shape
            count = lows[index].size
            from_lower = received[1][offset : offset + count].reshape(piece_shape)
            from_upper = received[-1][offset : offset + count].reshape(piece_shape)
            offset = offset + count
            grown.append(jnp.concatenate([from_lower, field, from_upper], axis=dim_index))
        current = grown
    return current


def smooth_merged(items):
    results = {}
    approxes = [damping * rhs / (6.0 * 0.25**lev) for rhs, lev in items]
    for sweep_index in range(SWEEPS - 1):
        padded_list = extend_all(approxes, 1)
        renewed = []
        for index, (rhs, lev) in enumerate(items):
            scaling = 0.25**lev
            diagonal_value = 6.0 * scaling
            renewed.append(
                approxes[index]
                + damping * (rhs - scaling * padded_stencil(padded_list[index])) / diagonal_value
            )
        approxes = renewed
    for index, (rhs, lev) in enumerate(items):
        results[lev] = approxes[index]
    return results


def precondition(residual):
    chain = [residual]
    for level_index in range(1, LEVELS):
        chain.append(restrict(chain[-1]))
    first_level = LEVELS - 1
    local_levels = list(range(first_level + 1))
    smoothed = smooth_merged([(chain[lev], lev) for lev in local_levels])
    correction = smoothed[first_level]
    for level_index in range(first_level - 1, -1, -1):
        correction = prolong(correction) + smoothed[level_index]
    return correction


def apply_fine(field):
    padded = padded_2(field, (("gx", 0), ("gy", 1), ("gz", 2)), 1)
    return padded_stencil(padded)


def shards(right_side, guess):
    solution_field = guess
    residual = right_side - apply_fine(guess)
    for step_index in range(STEPS):
        direction = precondition(residual)
        image = apply_fine(direction)
        along, curvature = lax.psum(
            (jnp.sum(residual * direction), jnp.sum(direction * image)), ("gx", "gy", "gz")
        )
        alpha = along / curvature
        solution_field = solution_field + alpha * direction
        residual = residual - alpha * image
    return (solution_field, residual)


def solution(mesh):
    placed = (P("gx", "gy", "gz"), P("gx", "gy", "gz"))
    return jax.shard_map(
        shards,
        mesh=mesh,
        in_specs=placed,
        out_specs=(P("gx", "gy", "gz"), P("gx", "gy", "gz")),
        check_vma=False,
    )
```

profile of v0, /device:TPU:0, one launch (start us, length us, event | category | flops | bytes accessed | tf_op | source)
XLA Modules:
  0.0 606.6 jit_solution(4249604036732145625)
XLA Ops:
  2.7 5.6 collective-permute-start.1
  11.0 3.0 collective-permute-start.3
  17.2 4.5 collective-permute-start.5
  23.5 1.8 broadcast_multiply_fusion.1
  25.7 34.9 %reshape.1638 = f32[16,2,16,2,64,2]{5,4,3,2,1,0:T(8,128)} reshape(f32[32,32,128]{2,1,0:T(8,128)S(1)} %copy.405) | data formatting | bytes 1048576 | tf_op jit(solution)/shard_map/reshape | solution.py:40
  60.5 12.2 %reduce_sum.140 = f32[16,16,64]{2,1,0:T(8,128)S(1)} reduce(f32[16,2,16,2,64,2]{5,4,3,2,1,0:T(8,128)} %reshape.1638, f32[]{:T(128)} %constant.169.clone.1), dimensions={1,3,5}, to_apply=%region_0.0 | reduce | flops 114688 | bytes 589828 | tf_op jit(solution)/shard_map/reduce_sum | solution.py:41
  72.8 5.6 div.223
  78.4 2.6 reduce_sum.141
  82.3 4.2 collective-permute-start.7
  88.3 4.3 collective-permute-done.6
  97.4 5.7 collective-permute-done.8
  109.0 4.7 collective-permute-start.11
  122.3 3.5 collective-permute-start.13
  128.3 4.4 collective-permute-done.12
  134.3 2.0 collective-permute-start.15
  138.2 3.5 collective-permute-done.14
  147.7 4.5 collective-permute-start.17
  163.2 3.5 collective-permute-start.19
  170.4 4.4 collective-permute-done.18
  176.4 2.0 collective-permute-start.21
  180.3 3.5 collective-permute-done.20
  190.2 4.9 collective-permute-start.23
  201.7 2.5 broadcast_in_dim.38
  204.2 4.9 reshape.1846
  210.7 11.4 %broadcast_in_dim.39 = f32[16,2,16,2,64,2]{5,4,3,2,1,0:T(8,128)} broadcast(f32[16,16,64]{2,1,0:T(8,128)S(1)} %fusion.112), dimensions={0,2,4} | broadcast | bytes 589824 | tf_op jit(solution)/shard_map/broadcast_in_dim | solution.py:46
  222.0 24.1 %reshape.1849 = f32[32,32,128]{2,1,0:T(8,128)S(1)} reshape(f32[16,2,16,2,64,2]{5,4,3,2,1,0:T(8,128)} %broadcast_in_dim.39) | data formatting | bytes 1048576 | tf_op jit(solution)/shard_map/reshape | solution.py:47
  247.1 1.5 fusion.45
  250.0 4.5 collective-permute-start.25
  257.3 3.0 collective-permute-start.27
  263.5 4.5 collective-permute-start.29
  271.1 45.0 %all-reduce.1 = (f32[]{:T(128)}, f32[]{:T(128)}) all-reduce(f32[]{:T(128)} %get-tuple-element.9, f32[]{:T(128)} %get-tuple-element.8), channel_id=1, replica_groups=mesh['gx'=4,'gy'=4,'gz'=2] {'gx','gy','gz'}, use_global_device_ids=true, to_apply=%region_7.0 | all-reduce | flops 2 | bytes 16 | tf_op jit(solution)/shard_map/psum | solution.py:127
  317.9 34.9 %reshape.1852 = f32[16,2,16,2,64,2]{5,4,3,2,1,0:T(8,128)} reshape(f32[32,32,128]{2,1,0:T(8,128)S(1)} %copy.511) | data formatting | bytes 1048576 | tf_op jit(solution)/shard_map/reshape | solution.py:40
  352.7 12.2 %reduce_sum.149 = f32[16,16,64]{2,1,0:T(8,128)S(1)} reduce(f32[16,2,16,2,64,2]{5,4,3,2,1,0:T(8,128)} %reshape.1852, f32[]{:T(128)} %constant.169.clone.1), dimensions={1,3,5}, to_apply=%region_10.0 | reduce | flops 114688 | bytes 589828 | tf_op jit(solution)/shard_map/reduce_sum | solution.py:41
  365.0 5.6 div.269
  370.6 2.6 reduce_sum.150
  374.5 1.8 collective-permute-start.31
  378.1 4.3 collective-permute-done.30
  387.2 4.3 collective-permute-done.32
  395.3 1.5 copy.517
  399.4 4.5 collective-permute-start.35
  410.0 1.7 fusion.29
  412.0 2.6 collective-permute-start.37
  416.4 4.3 collective-permute-done.36
  422.3 2.2 collective-permute-start.39
  424.9 1.5 collective-permute-start.38
  426.5 3.2 collective-permute-done.38
  437.6 4.5 collective-permute-start.41
  448.3 1.7 fusion.20
  450.2 3.9 collective-permute-start.43
  455.9 4.4 collective-permute-done.42
  461.9 2.0 collective-permute-start.45
  465.8 3.5 collective-permute-done.44
  477.2 4.8 collective-permute-start.47
  485.6 2.5 broadcast_in_dim.86
  488.1 4.9 reshape.2060
  493.8 11.4 %broadcast_in_dim.87 = f32[16,2,16,2,64,2]{5,4,3,2,1,0:T(8,128)} broadcast(f32[16,16,64]{2,1,0:T(8,128)S(1)} %fusion.81), dimensions={0,2,4} | broadcast | bytes 589824 | tf_op jit(solution)/shard_map/broadcast_in_dim | solution.py:46
  505.1 24.5 %reshape.2063 = f32[32,32,128]{2,1,0:T(8,128)} reshape(f32[16,2,16,2,64,2]{5,4,3,2,1,0:T(8,128)} %broadcast_in_dim.87) | data formatting | bytes 1048576 | tf_op jit(solution)/shard_map/reshape | solution.py:47
  530.6 1.9 fusion.11
  533.8 4.5 collective-permute-start.49
  541.1 3.0 collective-permute-start.51
  547.9 4.5 collective-permute-start.53
  554.3 2.1 multiply_reduce_fusion
  556.4 44.8 %all-reduce = (f32[]{:T(128)}, f32[]{:T(128)}) all-reduce(f32[]{:T(128)} %get-tuple-element.7, f32[]{:T(128)} %get-tuple-element.6), channel_id=1, replica_groups=mesh['gx'=4,'gy'=4,'gz'=2] {'gx','gy','gz'}, use_global_device_ids=true, to_apply=%region_17.0 | all-reduce | flops 2 | bytes 16 | tf_op jit(solution)/shard_map/psum | solution.py:127
  602.5 1.5 multiply_subtract_fusion
  (1008 shorter events, 155.5 us)
Async XLA Ops:
  1.4 8.2 %collective-permute-start = (f32[1,32,128]{2,0,1:T(1,128)S(1)}, f32[1,32,128]{2,0,1:T(1,128)S(1)}, u32[]{:S(2)}, u32[]{:S(2)}) collective-permute-start(f32[1,32,128]{2,0,1:T(1,128)S(1)} %bitcast.399), channel_id=1, source_target_pairs={{8,0},{16,8},{24,16},{9,1},{17,9},{25,17},{10,2},{18,10},{26,18},{... | collective-permute-start | bytes 49160 | tf_op jit(solution)/shard_map/ppermute | solution.py:26
  2.7 7.0 %collective-permute-start.1 = (f32[1,32,128]{2,0,1:T(1,128)S(1)}, f32[1,32,128]{2,0,1:T(1,128)S(1)}, u32[]{:S(2)}, u32[]{:S(2)}) collective-permute-start(f32[1,32,128]{2,0,1:T(1,128)S(1)} %bitcast.398), channel_id=1, source_target_pairs={{0,8},{8,16},{16,24},{1,9},{9,17},{17,25},{2,10},{10,18},{18,26},{... | collective-permute-start | bytes 49160 | tf_op jit(solution)/shard_map/ppermute | solution.py:25
  9.7 4.3 collective-permute-start.2
  11.0 3.9 collective-permute-start.3
  15.5 6.2 %collective-permute-start.4 = (f32[34,34,1]{1,2,0:T(1,128)S(1)}, f32[34,34,1]{1,2,0:T(1,128)S(1)}, u32[]{:S(2)}, u32[]{:S(2)}) collective-permute-start(f32[34,34,1]{1,2,0:T(1,128)S(1)} %copy.400), channel_id=1, source_target_pairs={{1,0},{3,2},{5,4},{7,6},{9,8},{11,10},{13,12},{15,14},{17,16},{19,... | collective-permute-start | bytes 13880 | tf_op jit(solution)/shard_map/ppermute | solution.py:26
  17.2 6.0 collective-permute-start.5
  81.6 74.1 %copy-start.7 = (f32[2,2,8]{2,1,0:T(2,128)}, f32[2,2,8]{2,1,0:T(2,128)S(1)}, u32[]{:S(2)}) copy-start(f32[2,2,8]{2,1,0:T(2,128)S(1)} %reduce_sum.143) | copy-start | bytes 388
  81.8 71.8 %copy-start.20 = (f32[4]{0:T(128)}, f32[4]{0:T(128)S(1)}, u32[]{:S(2)}) copy-start(f32[4]{0:T(128)S(1)} %reduce_sum.146) | copy-start | bytes 52
  82.3 5.9 collective-permute-start.7
  86.9 5.7 collective-permute-start.6
  88.3 14.9 %copy-start.21 = (f32[1,1,4]{2,1,0:T(1,128)}, f32[1,1,4]{2,1,0:T(1,128)S(1)}, u32[]{:S(2)}) copy-start(f32[1,1,4]{2,1,0:T(1,128)S(1)} %slice_bitcast_fusion.22) | copy-start | bytes 52
  94.2 3.0 collective-permute-start.9
  95.9 7.1 %collective-permute-start.8 = (f32[5964]{0:T(1024)S(1)}, f32[5964]{0:T(1024)S(1)}, u32[]{:S(2)}, u32[]{:S(2)}) collective-permute-start(f32[5964]{0:T(1024)S(1)} %concatenate.1027), channel_id=1, source_target_pairs={{2,0},{4,2},{6,4},{3,1},{5,3},{7,5},{10,8},{12,10},{14,12},{11,9},... | collective-permute-start | bytes 71576 | tf_op jit(solution)/shard_map/ppermute | solution.py:15
  106.6 7.2 %collective-permute-start.10 = (f32[1641]{0:T(1024)S(1)}, f32[1641]{0:T(1024)S(1)}, u32[]{:S(2)}, u32[]{:S(2)}) collective-permute-start(f32[1641]{0:T(1024)S(1)} %concatenate.1035), channel_id=1, source_target_pairs={{1,0},{3,2},{5,4},{7,6},{9,8},{11,10},{13,12},{15,14},{17,16},{19,... | collective-permute-start | bytes 19700 | tf_op jit(solution)/shard_map/ppermute | solution.py:15
  109.0 5.9 collective-permute-start.11
  121.6 22.0 %copy-start.17 = (f32[1,1,4]{2,1,0:T(1,128)}, f32[1,1,4]{2,1,0:T(1,128)S(1)}, u32[]{:S(2)}) copy-start(f32[1,1,4]{2,1,0:T(1,128)S(1)} %fusion.366) | copy-start | bytes 52
  122.3 5.9 collective-permute-start.13
  126.9 5.8 collective-permute-start.12
  134.3 3.7 collective-permute-start.15
  136.7 5.0 collective-permute-start.14
  138.0 22.4 %copy-start.10 = (f32[5964]{0:T(1024)}, f32[5964]{0:T(1024)S(1)}, u32[]{:S(2)}) copy-start(f32[5964]{0:T(1024)S(1)} %collective-permute-done.15) | copy-start | bytes 71572
  145.3 7.0 %collective-permute-start.16 = (f32[1641]{0:T(1024)S(1)}, f32[1641]{0:T(1024)S(1)}, u32[]{:S(2)}, u32[]{:S(2)}) collective-permute-start(f32[1641]{0:T(1024)S(1)} %concatenate.1085), channel_id=1, source_target_pairs={{1,0},{3,2},{5,4},{7,6},{9,8},{11,10},{13,12},{15,14},{17,16},{19,... | collective-permute-start | bytes 19700 | tf_op jit(solution)/shard_map/ppermute | solution.py:15
  147.7 5.9 collective-permute-start.17
  154.2 22.1 %copy-start.12 = (f32[2,2,8]{2,1,0:T(2,128)}, f32[2,2,8]{2,1,0:T(2,128)S(1)}, u32[]{:S(2)}) copy-start(f32[2,2,8]{2,1,0:T(2,128)S(1)} %multiply_add_fusion.3) | copy-start | bytes 388
  155.9 30.8 %copy-start.2 = (f32[4,4,16]{2,1,0:T(4,128)}, f32[4,4,16]{2,1,0:T(4,128)S(1)}, u32[]{:S(2)}) copy-start(f32[4,4,16]{2,1,0:T(4,128)S(1)} %fusion.258) | copy-start | bytes 3076
  163.2 7.2 %collective-permute-start.19 = (f32[5460]{0:T(1024)S(1)}, f32[5460]{0:T(1024)S(1)}, u32[]{:S(2)}, u32[]{:S(2)}) collective-permute-start(f32[5460]{0:T(1024)S(1)} %concatenate.1120), channel_id=1, source_target_pairs={{0,8},{8,16},{16,24},{1,9},{9,17},{17,25},{2,10},{10,18},{18,26},{... | collective-permute-start | bytes 65528 | tf_op jit(solution)/shard_map/ppermute | solution.py:15
  169.1 5.8 collective-permute-start.18
  176.4 3.7 collective-permute-start.21
  178.8 5.0 collective-permute-start.20
  186.3 14.3 %copy-start.3 = (f32[18,1,64]{2,1,0:T(1,128)}, f32[18,1,64]{2,1,0:T(1,128)S(1)}, u32[]{:S(2)}) copy-start(f32[18,1,64]{2,1,0:T(1,128)S(1)} %reshape.1817) | copy-start | bytes 13828
  186.4 14.2 %copy-start.4 = (f32[18,1,64]{2,1,0:T(1,128)}, f32[18,1,64]{2,1,0:T(1,128)S(1)}, u32[]{:S(2)}) copy-start(f32[18,1,64]{2,1,0:T(1,128)S(1)} %reshape.1818) | copy-start | bytes 13828
  187.7 7.4 %collective-permute-start.22 = (f32[1641]{0:T(1024)S(1)}, f32[1641]{0:T(1024)S(1)}, u32[]{:S(2)}, u32[]{:S(2)}) collective-permute-start(f32[1641]{0:T(1024)S(1)} %concatenate.1135), channel_id=1, source_target_pairs={{1,0},{3,2},{5,4},{7,6},{9,8},{11,10},{13,12},{15,14},{17,16},{19,... | collective-permute-start | bytes 19700 | tf_op jit(solution)/shard_map/ppermute | solution.py:15
  190.2 5.9 collective-permute-start.23
  248.7 5.9 collective-permute-start.24
  250.0 6.0 collective-permute-start.25
  256.0 4.3 collective-permute-start.26
  257.3 3.9 collective-permute-start.27
  261.8 6.2 %collective-permute-start.28 = (f32[34,34,1]{1,2,0:T(1,128)S(1)}, f32[34,34,1]{1,2,0:T(1,128)S(1)}, u32[]{:S(2)}, u32[]{:S(2)}) collective-permute-start(f32[34,34,1]{1,2,0:T(1,128)S(1)} %copy.506), channel_id=1, source_target_pairs={{1,0},{3,2},{5,4},{7,6},{9,8},{11,10},{13,12},{15,14},{17,16},{19,... | collective-permute-start | bytes 13880 | tf_op jit(solution)/shard_map/ppermute | solution.py:26
  263.5 6.0 collective-permute-start.29
  374.5 3.5 collective-permute-start.31
  376.8 5.7 collective-permute-start.30
  384.0 3.0 collective-permute-start.33
  385.7 5.8 collective-permute-start.32
  397.0 7.0 %collective-permute-start.34 = (f32[1641]{0:T(1024)S(1)}, f32[1641]{0:T(1024)S(1)}, u32[]{:S(2)}, u32[]{:S(2)}) collective-permute-start(f32[1641]{0:T(1024)S(1)} %concatenate.1193), channel_id=1, source_target_pairs={{1,0},{3,2},{5,4},{7,6},{9,8},{11,10},{13,12},{15,14},{17,16},{19,... | collective-permute-start | bytes 19700 | tf_op jit(solution)/shard_map/ppermute | solution.py:15
  399.4 5.9 collective-permute-start.35
  412.0 4.3 collective-permute-start.37
  415.0 5.7 collective-permute-start.36
  422.3 4.1 collective-permute-start.39
  424.9 4.9 collective-permute-start.38
  435.2 7.0 %collective-permute-start.40 = (f32[1641]{0:T(1024)S(1)}, f32[1641]{0:T(1024)S(1)}, u32[]{:S(2)}, u32[]{:S(2)}) collective-permute-start(f32[1641]{0:T(1024)S(1)} %concatenate.1243), channel_id=1, source_target_pairs={{1,0},{3,2},{5,4},{7,6},{9,8},{11,10},{13,12},{15,14},{17,16},{19,... | collective-permute-start | bytes 19700 | tf_op jit(solution)/shard_map/ppermute | solution.py:15
  437.6 5.9 collective-permute-start.41
  450.2 5.6 collective-permute-start.43
  454.5 5.8 collective-permute-start.42
  461.9 3.7 collective-permute-start.45
  464.3 5.0 collective-permute-start.44
  471.9 57.6 %copy-start.1 = (f32[34,1,128]{2,0,1:T(8,128)}, f32[34,1,128]{2,0,1:T(8,128)S(1)}, u32[]{:S(2)}) copy-start(f32[34,1,128]{2,0,1:T(8,128)S(1)} %slice_bitcast_fusion) | copy-start | bytes 52228
  474.8 7.2 %collective-permute-start.46 = (f32[1641]{0:T(1024)S(1)}, f32[1641]{0:T(1024)S(1)}, u32[]{:S(2)}, u32[]{:S(2)}) collective-permute-start(f32[1641]{0:T(1024)S(1)} %concatenate.1293), channel_id=1, source_target_pairs={{1,0},{3,2},{5,4},{7,6},{9,8},{11,10},{13,12},{15,14},{17,16},{19,... | collective-permute-start | bytes 19700 | tf_op jit(solution)/shard_map/ppermute | solution.py:15
  477.2 5.9 collective-permute-start.47
  532.5 5.9 collective-permute-start.48
  533.8 6.0 collective-permute-start.49
  539.8 4.3 collective-permute-start.50
  541.1 3.9 collective-permute-start.51
  546.2 6.2 %collective-permute-start.52 = (f32[34,34,1]{1,2,0:T(1,128)S(1)}, f32[34,34,1]{1,2,0:T(1,128)S(1)}, u32[]{:S(2)}, u32[]{:S(2)}) collective-permute-start(f32[34,34,1]{1,2,0:T(1,128)S(1)} %copy.612), channel_id=1, source_target_pairs={{1,0},{3,2},{5,4},{7,6},{9,8},{11,10},{13,12},{15,14},{17,16},{19,... | collective-permute-start | bytes 13880 | tf_op jit(solution)/shard_map/ppermute | solution.py:26
  547.9 6.0 collective-permute-start.53
  (15 other events, 103.3 us)
where the time goes:
time: 617 us; the launch traced here: 607 us
  local copies, waits for them, and re-layouts  258 us (42%)
  starting transfers between devices  131 us (21%)
  blocking collectives  89.7 us (15%)
  waiting for transfers between devices  64.4 us (10%)
  other arithmetic  57.4 us (9%)
  between operations  6.56 us (1%)
    psum x2, blocking collectives, shards(): lax.psum((jnp.sum(residual * direction), jnp.sum(direction * image)), ('g...  89.7 us
    ppermute x36, starting transfers between devices, passed_along(): lax.ppermute(value, axis, [(source, source + steps) for source in range(f...  81.6 us
    reshape x2, local copies, waits for them, and re-layouts, restrict(): blocks = field.reshape(first // 2, 2, second // 2, 2, third // 2, 2)  69.7 us
    reshape x8, local copies, waits for them, and re-layouts, prolong(): return spread.reshape(first * 2, second * 2, third * 2)  58.9 us
    ppermute x36, waiting for transfers between devices, passed_along(): lax.ppermute(value, axis, [(source, source + steps) for source in range(f...  56 us
    ppermute x9, starting transfers between devices, padded_2(): before = lax.ppermute(last, axis, up)  37.4 us
    reduce_sum x12, other arithmetic, restrict(): return jnp.mean(blocks, axis=(1, 3, 5))  30.3 us
    broadcast_in_dim x12, local copies, waits for them, and re-layouts, prolong(): jnp.broadcast_to(field[:, None, :, None, :, None], (first, 2, second, 2,...  28.4 us
  transfers between devices with their start and end apart: 54, of which 27 were waited for; matrix products, arithmetic and copies ran while one was open for 3% of the time, Pallas kernels for 0%

commit v1 on v0

--- a/solution.py
+++ b/solution.py
@@ -1,3 +1,4 @@
+import functools
 import jax
 import jax.numpy as jnp
 from jax import lax
@@ -7,6 +8,15 @@
 SWEEPS = 4
 STEPS = 2
 damping = 2.0 / 3.0
+
+
+def apply_space_on_mesh(u, peer_axis, device_axis):
+    for dev_i in (peer_axis, device_axis):
+        u = lax.psum(u, axis_name=dev_i)
+    return u
+
+
+group_the_shelves = functools.partial(apply_space_on_mesh, peer_axis="gx", device_axis=("gy", "gz"))
 
 
 def passed_along(value, axis, steps):
@@ -124,8 +134,8 @@
     for step_index in range(STEPS):
         direction = precondition(residual)
         image = apply_fine(direction)
-        along, curvature = lax.psum(
-            (jnp.sum(residual * direction), jnp.sum(direction * image)), ("gx", "gy", "gz")
+        along, curvature = group_the_shelves(
+            (jnp.sum(residual * direction), jnp.sum(direction * image))
         )
         alpha = along / curvature
         solution_field = solution_field + alpha * direction

time: 617 us -> 582 us (0.943)
  blocking collectives: 89.7 us -> 56.8 us
    psum x2 -> x4, blocking collectives: 89.7 us -> 56.8 us  [apply_space_on_mesh(): u = lax.psum(u, axis_name=dev_i)]
where the time goes in v1:
time: 582 us; the launch traced here: 572 us
  local copies, waits for them, and re-layouts  258 us (44%)
  starting transfers between devices  128 us (22%)
  waiting for transfers between devices  64.6 us (11%)
  other arithmetic  57.4 us (10%)
  blocking collectives  56.8 us (10%)
  between operations  6.5 us (1%)
    ppermute x36, starting transfers between devices, passed_along(): lax.ppermute(value, axis, [(source, source + steps) for source in range(f...  79.4 us
    reshape x2, local copies, waits for them, and re-layouts, restrict(): blocks = field.reshape(first // 2, 2, second // 2, 2, third // 2, 2)  69.7 us
    reshape x8, local copies, waits for them, and re-layouts, prolong(): return spread.reshape(first * 2, second * 2, third * 2)  58.9 us
    psum x4, blocking collectives, apply_space_on_mesh(): u = lax.psum(u, axis_name=dev_i)  56.8 us
    ppermute x36, waiting for transfers between devices, passed_along(): lax.ppermute(value, axis, [(source, source + steps) for source in range(f...  56.2 us
    ppermute x9, starting transfers between devices, padded_2(): before = lax.ppermute(last, axis, up)  37.4 us
    reduce_sum x12, other arithmetic, restrict(): return jnp.mean(blocks, axis=(1, 3, 5))  30.3 us
    broadcast_in_dim x12, local copies, waits for them, and re-layouts, prolong(): jnp.broadcast_to(field[:, None, :, None, :, None], (first, 2, second, 2,...  28.4 us
  transfers between devices with their start and end apart: 54, of which 27 were waited for; matrix products, arithmetic and copies ran while one was open for 3% of the time, Pallas kernels for 0%

profile of v1, /device:TPU:0, one launch (start us, length us, event | category | flops | bytes accessed | tf_op | source)
XLA Modules:
  0.0 571.6 jit_solution(3017431412340355313)
XLA Ops:
  2.7 5.6 collective-permute-start.1
  11.0 3.0 collective-permute-start.3
  17.2 4.5 collective-permute-start.5
  23.5 1.8 broadcast_multiply_fusion.1
  25.7 34.9 %reshape.1638 = f32[16,2,16,2,64,2]{5,4,3,2,1,0:T(8,128)} reshape(f32[32,32,128]{2,1,0:T(8,128)S(1)} %copy.405) | data formatting | bytes 1048576 | tf_op jit(solution)/shard_map/reshape | solution.py:50
  60.5 12.2 %reduce_sum.140 = f32[16,16,64]{2,1,0:T(8,128)S(1)} reduce(f32[16,2,16,2,64,2]{5,4,3,2,1,0:T(8,128)} %reshape.1638, f32[]{:T(128)} %constant.169.clone.1), dimensions={1,3,5}, to_apply=%region_0.0 | reduce | flops 114688 | bytes 589828 | tf_op jit(solution)/shard_map/reduce_sum | solution.py:51
  72.8 5.6 div.223
  78.4 2.6 reduce_sum.141
  82.3 4.2 collective-permute-start.7
  88.3 4.3 collective-permute-done.6
  97.4 5.7 collective-permute-done.8
  109.0 4.7 collective-permute-start.11
  122.3 3.5 collective-permute-start.13
  128.3 4.4 collective-permute-done.12
  134.3 2.0 collective-permute-start.15
  138.2 3.5 collective-permute-done.14
  147.7 4.5 collective-permute-start.17
  163.2 3.5 collective-permute-start.19
  170.4 4.4 collective-permute-done.18
  176.4 2.0 collective-permute-start.21
  180.3 3.5 collective-permute-done.20
  190.2 4.9 collective-permute-start.23
  201.7 2.5 broadcast_in_dim.38
  204.2 4.9 reshape.1846
  210.7 11.4 %broadcast_in_dim.39 = f32[16,2,16,2,64,2]{5,4,3,2,1,0:T(8,128)} broadcast(f32[16,16,64]{2,1,0:T(8,128)S(1)} %fusion.112), dimensions={0,2,4} | broadcast | bytes 589824 | tf_op jit(solution)/shard_map/broadcast_in_dim | solution.py:56
  222.0 24.1 %reshape.1849 = f32[32,32,128]{2,1,0:T(8,128)S(1)} reshape(f32[16,2,16,2,64,2]{5,4,3,2,1,0:T(8,128)} %broadcast_in_dim.39) | data formatting | bytes 1048576 | tf_op jit(solution)/shard_map/reshape | solution.py:57
  247.1 1.5 fusion.45
  250.0 4.5 collective-permute-start.25
  257.3 3.0 collective-permute-start.27
  263.5 4.5 collective-permute-start.29
  271.1 11.3 %all-reduce.3 = (f32[]{:T(128)}, f32[]{:T(128)}) all-reduce(f32[]{:T(128)} %get-tuple-element.9, f32[]{:T(128)} %get-tuple-element.8), channel_id=1, replica_groups=mesh['gx'=4,'gy'=4,'gz'=2] {'gx'}, use_global_device_ids=true, to_apply=%region_7.0 | all-reduce | flops 2 | bytes 16 | tf_op jit(solution)/shard_map/psum | solution.py:15
  282.5 17.1 %all-reduce.1 = (f32[]{:T(128)}, f32[]{:T(128)}) all-reduce(f32[]{:T(128)} %get-tuple-element.100, f32[]{:T(128)} %get-tuple-element.101), channel_id=1, replica_groups=mesh['gx'=4,'gy'=4,'gz'=2] {'gy','gz'}, use_global_device_ids=true, to_apply=%region_8.0 | all-reduce | flops 2 | bytes 16 | tf_op jit(solution)/shard_map/psum | solution.py:15
  301.4 34.9 %reshape.1852 = f32[16,2,16,2,64,2]{5,4,3,2,1,0:T(8,128)} reshape(f32[32,32,128]{2,1,0:T(8,128)S(1)} %copy.511) | data formatting | bytes 1048576 | tf_op jit(solution)/shard_map/reshape | solution.py:50
  336.3 12.2 %reduce_sum.149 = f32[16,16,64]{2,1,0:T(8,128)S(1)} reduce(f32[16,2,16,2,64,2]{5,4,3,2,1,0:T(8,128)} %reshape.1852, f32[]{:T(128)} %constant.169.clone.1), dimensions={1,3,5}, to_apply=%region_12.0 | reduce | flops 114688 | bytes 589828 | tf_op jit(solution)/shard_map/reduce_sum | solution.py:51
  348.5 5.6 div.269
  354.1 2.6 reduce_sum.150
  358.0 1.6 collective-permute-start.31
  361.4 4.3 collective-permute-done.30
  370.4 3.9 collective-permute-done.32
  382.3 4.5 collective-permute-start.35
  392.9 1.7 fusion.29
  394.9 2.4 collective-permute-start.37
  399.0 4.4 collective-permute-done.36
  405.0 2.0 collective-permute-start.39
  408.9 3.5 collective-permute-done.38
  417.9 1.5 collective-permute-start.40
  420.5 4.5 collective-permute-start.41
  431.2 1.7 fusion.20
  433.1 2.6 collective-permute-start.43
  437.5 4.4 collective-permute-done.42
  443.4 2.0 collective-permute-start.45
  447.3 3.5 collective-permute-done.44
  458.7 4.5 collective-permute-start.47
  467.1 2.5 broadcast_in_dim.86
  469.6 4.9 reshape.2060
  475.3 11.4 %broadcast_in_dim.87 = f32[16,2,16,2,64,2]{5,4,3,2,1,0:T(8,128)} broadcast(f32[16,16,64]{2,1,0:T(8,128)S(1)} %fusion.81), dimensions={0,2,4} | broadcast | bytes 589824 | tf_op jit(solution)/shard_map/broadcast_in_dim | solution.py:56
  486.7 24.5 %reshape.2063 = f32[32,32,128]{2,1,0:T(8,128)} reshape(f32[16,2,16,2,64,2]{5,4,3,2,1,0:T(8,128)} %broadcast_in_dim.87) | data formatting | bytes 1048576 | tf_op jit(solution)/shard_map/reshape | solution.py:57
  512.1 1.9 fusion.11
  515.3 4.5 collective-permute-start.49
  522.6 3.0 collective-permute-start.51
  529.4 4.5 collective-permute-start.53
  535.8 2.1 multiply_reduce_fusion
  537.9 11.3 %all-reduce.2 = (f32[]{:T(128)}, f32[]{:T(128)}) all-reduce(f32[]{:T(128)} %get-tuple-element.7, f32[]{:T(128)} %get-tuple-element.6), channel_id=1, replica_groups=mesh['gx'=4,'gy'=4,'gz'=2] {'gx'}, use_global_device_ids=true, to_apply=%region_19.0 | all-reduce | flops 2 | bytes 16 | tf_op jit(solution)/shard_map/psum | solution.py:15
  549.2 17.0 %all-reduce = (f32[]{:T(128)}, f32[]{:T(128)}) all-reduce(f32[]{:T(128)} %get-tuple-element.98, f32[]{:T(128)} %get-tuple-element.99), channel_id=1, replica_groups=mesh['gx'=4,'gy'=4,'gz'=2] {'gy','gz'}, use_global_device_ids=true, to_apply=%region_20.0 | all-reduce | flops 2 | bytes 16 | tf_op jit(solution)/shard_map/psum | solution.py:15
  (1010 shorter events, 158.8 us)
Async XLA Ops:
  1.4 8.2 %collective-permute-start = (f32[1,32,128]{2,0,1:T(1,128)S(1)}, f32[1,32,128]{2,0,1:T(1,128)S(1)}, u32[]{:S(2)}, u32[]{:S(2)}) collective-permute-start(f32[1,32,128]{2,0,1:T(1,128)S(1)} %bitcast.399), channel_id=1, source_target_pairs={{8,0},{16,8},{24,16},{9,1},{17,9},{25,17},{10,2},{18,10},{26,18},{... | collective-permute-start | bytes 49160 | tf_op jit(solution)/shard_map/ppermute | solution.py:36
  2.7 7.0 %collective-permute-start.1 = (f32[1,32,128]{2,0,1:T(1,128)S(1)}, f32[1,32,128]{2,0,1:T(1,128)S(1)}, u32[]{:S(2)}, u32[]{:S(2)}) collective-permute-start(f32[1,32,128]{2,0,1:T(1,128)S(1)} %bitcast.398), channel_id=1, source_target_pairs={{0,8},{8,16},{16,24},{1,9},{9,17},{17,25},{2,10},{10,18},{18,26},{... | collective-permute-start | bytes 49160 | tf_op jit(solution)/shard_map/ppermute | solution.py:35
  9.7 4.3 collective-permute-start.2
  11.0 3.9 collective-permute-start.3
  15.5 6.2 %collective-permute-start.4 = (f32[34,34,1]{1,2,0:T(1,128)S(1)}, f32[34,34,1]{1,2,0:T(1,128)S(1)}, u32[]{:S(2)}, u32[]{:S(2)}) collective-permute-start(f32[34,34,1]{1,2,0:T(1,128)S(1)} %copy.400), channel_id=1, source_target_pairs={{1,0},{3,2},{5,4},{7,6},{9,8},{11,10},{13,12},{15,14},{17,16},{19,... | collective-permute-start | bytes 13880 | tf_op jit(solution)/shard_map/ppermute | solution.py:36
  17.2 6.0 %collective-permute-start.5 = (f32[34,34,1]{1,2,0:T(1,128)S(1)}, f32[34,34,1]{1,2,0:T(1,128)S(1)}, u32[]{:S(2)}, u32[]{:S(2)}) collective-permute-start(f32[34,34,1]{1,2,0:T(1,128)S(1)} %copy.402), channel_id=1, source_target_pairs={{0,1},{2,3},{4,5},{6,7},{8,9},{10,11},{12,13},{14,15},{16,17},{18,... | collective-permute-start | bytes 13880 | tf_op jit(solution)/shard_map/ppermute | solution.py:35
  81.6 74.1 %copy-start.7 = (f32[2,2,8]{2,1,0:T(2,128)}, f32[2,2,8]{2,1,0:T(2,128)S(1)}, u32[]{:S(2)}) copy-start(f32[2,2,8]{2,1,0:T(2,128)S(1)} %reduce_sum.143) | copy-start | bytes 388
  81.8 71.8 %copy-start.20 = (f32[4]{0:T(128)}, f32[4]{0:T(128)S(1)}, u32[]{:S(2)}) copy-start(f32[4]{0:T(128)S(1)} %reduce_sum.146) | copy-start | bytes 52
  82.3 5.9 %collective-permute-start.7 = (f32[5460]{0:T(1024)S(1)}, f32[5460]{0:T(1024)S(1)}, u32[]{:S(2)}, u32[]{:S(2)}) collective-permute-start(f32[5460]{0:T(1024)S(1)} %concatenate.1020), channel_id=1, source_target_pairs={{0,8},{8,16},{16,24},{1,9},{9,17},{17,25},{2,10},{10,18},{18,26},{... | collective-permute-start | bytes 65528 | tf_op jit(solution)/shard_map/ppermute | solution.py:25
  86.9 5.7 collective-permute-start.6
  88.3 14.9 %copy-start.21 = (f32[1,1,4]{2,1,0:T(1,128)}, f32[1,1,4]{2,1,0:T(1,128)S(1)}, u32[]{:S(2)}) copy-start(f32[1,1,4]{2,1,0:T(1,128)S(1)} %slice_bitcast_fusion.22) | copy-start | bytes 52
  94.2 3.0 collective-permute-start.9
  95.9 7.1 %collective-permute-start.8 = (f32[5964]{0:T(1024)S(1)}, f32[5964]{0:T(1024)S(1)}, u32[]{:S(2)}, u32[]{:S(2)}) collective-permute-start(f32[5964]{0:T(1024)S(1)} %concatenate.1027), channel_id=1, source_target_pairs={{2,0},{4,2},{6,4},{3,1},{5,3},{7,5},{10,8},{12,10},{14,12},{11,9},... | collective-permute-start | bytes 71576 | tf_op jit(solution)/shard_map/ppermute | solution.py:25
  106.6 7.2 %collective-permute-start.10 = (f32[1641]{0:T(1024)S(1)}, f32[1641]{0:T(1024)S(1)}, u32[]{:S(2)}, u32[]{:S(2)}) collective-permute-start(f32[1641]{0:T(1024)S(1)} %concatenate.1035), channel_id=1, source_target_pairs={{1,0},{3,2},{5,4},{7,6},{9,8},{11,10},{13,12},{15,14},{17,16},{19,... | collective-permute-start | bytes 19700 | tf_op jit(solution)/shard_map/ppermute | solution.py:25
  109.0 5.9 %collective-permute-start.11 = (f32[1641]{0:T(1024)S(1)}, f32[1641]{0:T(1024)S(1)}, u32[]{:S(2)}, u32[]{:S(2)}) collective-permute-start(f32[1641]{0:T(1024)S(1)} %concatenate.1037), channel_id=1, source_target_pairs={{0,1},{2,3},{4,5},{6,7},{8,9},{10,11},{12,13},{14,15},{16,17},{18,... | collective-permute-start | bytes 19700 | tf_op jit(solution)/shard_map/ppermute | solution.py:25
  121.6 22.0 %copy-start.17 = (f32[1,1,4]{2,1,0:T(1,128)}, f32[1,1,4]{2,1,0:T(1,128)S(1)}, u32[]{:S(2)}) copy-start(f32[1,1,4]{2,1,0:T(1,128)S(1)} %fusion.366) | copy-start | bytes 52
  122.3 5.9 %collective-permute-start.13 = (f32[5460]{0:T(1024)S(1)}, f32[5460]{0:T(1024)S(1)}, u32[]{:S(2)}, u32[]{:S(2)}) collective-permute-start(f32[5460]{0:T(1024)S(1)} %concatenate.1070), channel_id=1, source_target_pairs={{0,8},{8,16},{16,24},{1,9},{9,17},{17,25},{2,10},{10,18},{18,26},{... | collective-permute-start | bytes 65528 | tf_op jit(solution)/shard_map/ppermute | solution.py:25
  126.9 5.8 %collective-permute-start.12 = (f32[5460]{0:T(1024)S(1)}, f32[5460]{0:T(1024)S(1)}, u32[]{:S(2)}, u32[]{:S(2)}) collective-permute-start(f32[5460]{0:T(1024)S(1)} %concatenate.1069), channel_id=1, source_target_pairs={{8,0},{16,8},{24,16},{9,1},{17,9},{25,17},{10,2},{18,10},{26,18},{... | collective-permute-start | bytes 65528 | tf_op jit(solution)/shard_map/ppermute | solution.py:25
  134.3 3.7 collective-permute-start.15
  136.7 5.0 collective-permute-start.14
  138.0 22.4 %copy-start.10 = (f32[5964]{0:T(1024)}, f32[5964]{0:T(1024)S(1)}, u32[]{:S(2)}) copy-start(f32[5964]{0:T(1024)S(1)} %collective-permute-done.15) | copy-start | bytes 71572
  145.3 7.0 %collective-permute-start.16 = (f32[1641]{0:T(1024)S(1)}, f32[1641]{0:T(1024)S(1)}, u32[]{:S(2)}, u32[]{:S(2)}) collective-permute-start(f32[1641]{0:T(1024)S(1)} %concatenate.1085), channel_id=1, source_target_pairs={{1,0},{3,2},{5,4},{7,6},{9,8},{11,10},{13,12},{15,14},{17,16},{19,... | collective-permute-start | bytes 19700 | tf_op jit(solution)/shard_map/ppermute | solution.py:25
  147.7 5.9 %collective-permute-start.17 = (f32[1641]{0:T(1024)S(1)}, f32[1641]{0:T(1024)S(1)}, u32[]{:S(2)}, u32[]{:S(2)}) collective-permute-start(f32[1641]{0:T(1024)S(1)} %concatenate.1087), channel_id=1, source_target_pairs={{0,1},{2,3},{4,5},{6,7},{8,9},{10,11},{12,13},{14,15},{16,17},{18,... | collective-permute-start | bytes 19700 | tf_op jit(solution)/shard_map/ppermute | solution.py:25
  154.2 22.1 %copy-start.12 = (f32[2,2,8]{2,1,0:T(2,128)}, f32[2,2,8]{2,1,0:T(2,128)S(1)}, u32[]{:S(2)}) copy-start(f32[2,2,8]{2,1,0:T(2,128)S(1)} %multiply_add_fusion.3) | copy-start | bytes 388
  155.9 30.8 %copy-start.2 = (f32[4,4,16]{2,1,0:T(4,128)}, f32[4,4,16]{2,1,0:T(4,128)S(1)}, u32[]{:S(2)}) copy-start(f32[4,4,16]{2,1,0:T(4,128)S(1)} %fusion.258) | copy-start | bytes 3076
  163.2 7.2 %collective-permute-start.19 = (f32[5460]{0:T(1024)S(1)}, f32[5460]{0:T(1024)S(1)}, u32[]{:S(2)}, u32[]{:S(2)}) collective-permute-start(f32[5460]{0:T(1024)S(1)} %concatenate.1120), channel_id=1, source_target_pairs={{0,8},{8,16},{16,24},{1,9},{9,17},{17,25},{2,10},{10,18},{18,26},{... | collective-permute-start | bytes 65528 | tf_op jit(solution)/shard_map/ppermute | solution.py:25
  169.1 5.8 %collective-permute-start.18 = (f32[5460]{0:T(1024)S(1)}, f32[5460]{0:T(1024)S(1)}, u32[]{:S(2)}, u32[]{:S(2)}) collective-permute-start(f32[5460]{0:T(1024)S(1)} %concatenate.1119), channel_id=1, source_target_pairs={{8,0},{16,8},{24,16},{9,1},{17,9},{25,17},{10,2},{18,10},{26,18},{... | collective-permute-start | bytes 65528 | tf_op jit(solution)/shard_map/ppermute | solution.py:25
  176.4 3.7 collective-permute-start.21
  178.8 5.0 collective-permute-start.20
  186.3 14.3 %copy-start.3 = (f32[18,1,64]{2,1,0:T(1,128)}, f32[18,1,64]{2,1,0:T(1,128)S(1)}, u32[]{:S(2)}) copy-start(f32[18,1,64]{2,1,0:T(1,128)S(1)} %reshape.1817) | copy-start | bytes 13828
  186.4 14.2 %copy-start.4 = (f32[18,1,64]{2,1,0:T(1,128)}, f32[18,1,64]{2,1,0:T(1,128)S(1)}, u32[]{:S(2)}) copy-start(f32[18,1,64]{2,1,0:T(1,128)S(1)} %reshape.1818) | copy-start | bytes 13828
  187.7 7.4 %collective-permute-start.22 = (f32[1641]{0:T(1024)S(1)}, f32[1641]{0:T(1024)S(1)}, u32[]{:S(2)}, u32[]{:S(2)}) collective-permute-start(f32[1641]{0:T(1024)S(1)} %concatenate.1135), channel_id=1, source_target_pairs={{1,0},{3,2},{5,4},{7,6},{9,8},{11,10},{13,12},{15,14},{17,16},{19,... | collective-permute-start | bytes 19700 | tf_op jit(solution)/shard_map/ppermute | solution.py:25
  190.2 5.9 %collective-permute-start.23 = (f32[1641]{0:T(1024)S(1)}, f32[1641]{0:T(1024)S(1)}, u32[]{:S(2)}, u32[]{:S(2)}) collective-permute-start(f32[1641]{0:T(1024)S(1)} %concatenate.1137), channel_id=1, source_target_pairs={{0,1},{2,3},{4,5},{6,7},{8,9},{10,11},{12,13},{14,15},{16,17},{18,... | collective-permute-start | bytes 19700 | tf_op jit(solution)/shard_map/ppermute | solution.py:25
  248.7 5.9 %collective-permute-start.24 = (f32[1,32,128]{2,0,1:T(1,128)S(1)}, f32[1,32,128]{2,0,1:T(1,128)S(1)}, u32[]{:S(2)}, u32[]{:S(2)}) collective-permute-start(f32[1,32,128]{2,0,1:T(1,128)S(1)} %get-tuple-element.153), channel_id=1, source_target_pairs={{8,0},{16,8},{24,16},{9,1},{17,9},{25,17},{10,2},{18,10},{26,18},{... | collective-permute-start | bytes 49160 | tf_op jit(solution)/shard_map/ppermute | solution.py:36
  250.0 6.0 %collective-permute-start.25 = (f32[1,32,128]{2,0,1:T(1,128)S(1)}, f32[1,32,128]{2,0,1:T(1,128)S(1)}, u32[]{:S(2)}, u32[]{:S(2)}) collective-permute-start(f32[1,32,128]{2,0,1:T(1,128)S(1)} %get-tuple-element.152), channel_id=1, source_target_pairs={{0,8},{8,16},{16,24},{1,9},{9,17},{17,25},{2,10},{10,18},{18,26},{... | collective-permute-start | bytes 49160 | tf_op jit(solution)/shard_map/ppermute | solution.py:35
  256.0 4.3 collective-permute-start.26
  257.3 3.9 collective-permute-start.27
  261.8 6.2 %collective-permute-start.28 = (f32[34,34,1]{1,2,0:T(1,128)S(1)}, f32[34,34,1]{1,2,0:T(1,128)S(1)}, u32[]{:S(2)}, u32[]{:S(2)}) collective-permute-start(f32[34,34,1]{1,2,0:T(1,128)S(1)} %copy.506), channel_id=1, source_target_pairs={{1,0},{3,2},{5,4},{7,6},{9,8},{11,10},{13,12},{15,14},{17,16},{19,... | collective-permute-start | bytes 13880 | tf_op jit(solution)/shard_map/ppermute | solution.py:36
  263.5 6.0 %collective-permute-start.29 = (f32[34,34,1]{1,2,0:T(1,128)S(1)}, f32[34,34,1]{1,2,0:T(1,128)S(1)}, u32[]{:S(2)}, u32[]{:S(2)}) collective-permute-start(f32[34,34,1]{1,2,0:T(1,128)S(1)} %copy.508), channel_id=1, source_target_pairs={{0,1},{2,3},{4,5},{6,7},{8,9},{10,11},{12,13},{14,15},{16,17},{18,... | collective-permute-start | bytes 13880 | tf_op jit(solution)/shard_map/ppermute | solution.py:35
  358.0 3.3 collective-permute-start.31
  360.0 5.7 collective-permute-start.30
  367.3 3.0 collective-permute-start.33
  369.0 5.4 collective-permute-start.32
  379.9 7.0 %collective-permute-start.34 = (f32[1641]{0:T(1024)S(1)}, f32[1641]{0:T(1024)S(1)}, u32[]{:S(2)}, u32[]{:S(2)}) collective-permute-start(f32[1641]{0:T(1024)S(1)} %concatenate.1193), channel_id=1, source_target_pairs={{1,0},{3,2},{5,4},{7,6},{9,8},{11,10},{13,12},{15,14},{17,16},{19,... | collective-permute-start | bytes 19700 | tf_op jit(solution)/shard_map/ppermute | solution.py:25
  382.3 5.9 %collective-permute-start.35 = (f32[1641]{0:T(1024)S(1)}, f32[1641]{0:T(1024)S(1)}, u32[]{:S(2)}, u32[]{:S(2)}) collective-permute-start(f32[1641]{0:T(1024)S(1)} %concatenate.1195), channel_id=1, source_target_pairs={{0,1},{2,3},{4,5},{6,7},{8,9},{10,11},{12,13},{14,15},{16,17},{18,... | collective-permute-start | bytes 19700 | tf_op jit(solution)/shard_map/ppermute | solution.py:25
  394.9 4.1 collective-permute-start.37
  397.7 5.8 %collective-permute-start.36 = (f32[5460]{0:T(1024)S(1)}, f32[5460]{0:T(1024)S(1)}, u32[]{:S(2)}, u32[]{:S(2)}) collective-permute-start(f32[5460]{0:T(1024)S(1)} %concatenate.1227), channel_id=1, source_target_pairs={{8,0},{16,8},{24,16},{9,1},{17,9},{25,17},{10,2},{18,10},{26,18},{... | collective-permute-start | bytes 65528 | tf_op jit(solution)/shard_map/ppermute | solution.py:25
  405.0 3.7 collective-permute-start.39
  407.4 5.0 collective-permute-start.38
  417.9 7.2 %collective-permute-start.40 = (f32[1641]{0:T(1024)S(1)}, f32[1641]{0:T(1024)S(1)}, u32[]{:S(2)}, u32[]{:S(2)}) collective-permute-start(f32[1641]{0:T(1024)S(1)} %concatenate.1243), channel_id=1, source_target_pairs={{1,0},{3,2},{5,4},{7,6},{9,8},{11,10},{13,12},{15,14},{17,16},{19,... | collective-permute-start | bytes 19700 | tf_op jit(solution)/shard_map/ppermute | solution.py:25
  420.5 5.9 %collective-permute-start.41 = (f32[1641]{0:T(1024)S(1)}, f32[1641]{0:T(1024)S(1)}, u32[]{:S(2)}, u32[]{:S(2)}) collective-permute-start(f32[1641]{0:T(1024)S(1)} %concatenate.1245), channel_id=1, source_target_pairs={{0,1},{2,3},{4,5},{6,7},{8,9},{10,11},{12,13},{14,15},{16,17},{18,... | collective-permute-start | bytes 19700 | tf_op jit(solution)/shard_map/ppermute | solution.py:25
  433.1 4.3 collective-permute-start.43
  436.1 5.8 %collective-permute-start.42 = (f32[5460]{0:T(1024)S(1)}, f32[5460]{0:T(1024)S(1)}, u32[]{:S(2)}, u32[]{:S(2)}) collective-permute-start(f32[5460]{0:T(1024)S(1)} %concatenate.1277), channel_id=1, source_target_pairs={{8,0},{16,8},{24,16},{9,1},{17,9},{25,17},{10,2},{18,10},{26,18},{... | collective-permute-start | bytes 65528 | tf_op jit(solution)/shard_map/ppermute | solution.py:25
  443.4 3.7 collective-permute-start.45
  445.9 5.0 collective-permute-start.44
  453.5 57.6 %copy-start.1 = (f32[34,1,128]{2,0,1:T(8,128)}, f32[34,1,128]{2,0,1:T(8,128)S(1)}, u32[]{:S(2)}) copy-start(f32[34,1,128]{2,0,1:T(8,128)S(1)} %slice_bitcast_fusion) | copy-start | bytes 52228
  456.3 7.0 %collective-permute-start.46 = (f32[1641]{0:T(1024)S(1)}, f32[1641]{0:T(1024)S(1)}, u32[]{:S(2)}, u32[]{:S(2)}) collective-permute-start(f32[1641]{0:T(1024)S(1)} %concatenate.1293), channel_id=1, source_target_pairs={{1,0},{3,2},{5,4},{7,6},{9,8},{11,10},{13,12},{15,14},{17,16},{19,... | collective-permute-start | bytes 19700 | tf_op jit(solution)/shard_map/ppermute | solution.py:25
  458.7 5.9 %collective-permute-start.47 = (f32[1641]{0:T(1024)S(1)}, f32[1641]{0:T(1024)S(1)}, u32[]{:S(2)}, u32[]{:S(2)}) collective-permute-start(f32[1641]{0:T(1024)S(1)} %concatenate.1295), channel_id=1, source_target_pairs={{0,1},{2,3},{4,5},{6,7},{8,9},{10,11},{12,13},{14,15},{16,17},{18,... | collective-permute-start | bytes 19700 | tf_op jit(solution)/shard_map/ppermute | solution.py:25
  514.0 5.9 %collective-permute-start.48 = (f32[1,32,128]{2,0,1:T(1,128)S(1)}, f32[1,32,128]{2,0,1:T(1,128)S(1)}, u32[]{:S(2)}, u32[]{:S(2)}) collective-permute-start(f32[1,32,128]{2,0,1:T(1,128)S(1)} %get-tuple-element.145), channel_id=1, source_target_pairs={{8,0},{16,8},{24,16},{9,1},{17,9},{25,17},{10,2},{18,10},{26,18},{... | collective-permute-start | bytes 49160 | tf_op jit(solution)/shard_map/ppermute | solution.py:36
  515.3 6.0 %collective-permute-start.49 = (f32[1,32,128]{2,0,1:T(1,128)S(1)}, f32[1,32,128]{2,0,1:T(1,128)S(1)}, u32[]{:S(2)}, u32[]{:S(2)}) collective-permute-start(f32[1,32,128]{2,0,1:T(1,128)S(1)} %get-tuple-element.144), channel_id=1, source_target_pairs={{0,8},{8,16},{16,24},{1,9},{9,17},{17,25},{2,10},{10,18},{18,26},{... | collective-permute-start | bytes 49160 | tf_op jit(solution)/shard_map/ppermute | solution.py:35
  521.3 4.3 collective-permute-start.50
  522.6 3.9 collective-permute-start.51
  527.8 6.2 %collective-permute-start.52 = (f32[34,34,1]{1,2,0:T(1,128)S(1)}, f32[34,34,1]{1,2,0:T(1,128)S(1)}, u32[]{:S(2)}, u32[]{:S(2)}) collective-permute-start(f32[34,34,1]{1,2,0:T(1,128)S(1)} %copy.612), channel_id=1, source_target_pairs={{1,0},{3,2},{5,4},{7,6},{9,8},{11,10},{13,12},{15,14},{17,16},{19,... | collective-permute-start | bytes 13880 | tf_op jit(solution)/shard_map/ppermute | solution.py:36
  529.4 6.0 %collective-permute-start.53 = (f32[34,34,1]{1,2,0:T(1,128)S(1)}, f32[34,34,1]{1,2,0:T(1,128)S(1)}, u32[]{:S(2)}, u32[]{:S(2)}) collective-permute-start(f32[34,34,1]{1,2,0:T(1,128)S(1)} %copy.614), channel_id=1, source_target_pairs={{0,1},{2,3},{4,5},{6,7},{8,9},{10,11},{12,13},{14,15},{16,17},{18,... | collective-permute-start | bytes 13880 | tf_op jit(solution)/shard_map/ppermute | solution.py:35
  (15 other events, 103.3 us)
